TPU v7x, 32 devices: a whole 2x2x4 slice. The times are simulated.
32 devices in a mesh: row: 16 (over z, y, x), col: 2 (over core).
Axes of the slice: x: 2, y: 2, z: 4, core: 2. Of those that a mesh axis runs over, the one named last changes fastest.
Arguments:
- eri_cols: float32 [8192, 512], P('row'), as said below
- old_factor: float32 [8192, 1024], P('row', 'col')
- residual_diag: float32 [8192], P('row'), as said below
- pivots: int32 [4, 128], replicated, may hold values from 0 to 8191, as said below
- row_ids: int32 [8192], P('row'), may hold values from 0 to 8191, as said below
Outputs:
- panels: float32 [8192, 512], P('row')
- new_diag: float32 [8192], P('row')
Inputs may be any that keep to these rules, and one draw needn't show every extreme that they name: `pivots`: 512 distinct pair indices, each held by some stored row. `row_ids`: every pair index held by exactly one stored row. `eri_cols`: the pair matrix minus the earlier factor's product is symmetric positive definite on the pivots, with smallest eigenvalue 0.25 or more. `residual_diag`: the diagonal of the same residual matrix whose pivot columns eri_cols holds.
All inputs are finite; a program needn't handle non-finite values.
Results may differ from a plain program's by a relative error of at most 0.0003.
Values sent between devices are 32-bit elements; how exact they have to be, the bound alone decides.
A program may use at most 64 MiB of HBM per device.

v0:
```python
import jax
import jax.numpy as jnp
from jax import lax
from jax.sharding import PartitionSpec as P


def pick_rows(wanted, row_ids, arrays):
    matches = wanted[:, None] == row_ids[None, :]
    slots = jnp.sum(
        jnp.where(matches, lax.broadcasted_iota(jnp.int32, matches.shape, 1), 0), axis=1
    )
    present = jnp.any(matches, axis=1)[:, None]
    return tuple((jnp.where(present, jnp.take(source, slots, axis=0), 0.0) for source in arrays))


def product(left, right):
    return jnp.dot(
        left, right.T, precision=lax.Precision.HIGHEST, preferred_element_type=jnp.float32
    )


def solve_panel(factor_block, columns):
    return lax.linalg.triangular_solve(
        factor_block, columns, left_side=False, lower=True, transpose_a=True
    )


def on_device(eri_cols, old_factor, residual_diag, pivots, row_ids):
    steps = pivots.shape[0]
    width = pivots.shape[1]
    diagonal = residual_diag
    outputs = []
    every_pivot = pivots.reshape(-1)
    old_rows, eri_rows = pick_rows(every_pivot, row_ids, (old_factor, eri_cols))
    old_rows, eri_rows = lax.psum((old_rows, eri_rows), "row")
    old_cross, old_gram = lax.psum(
        (product(old_factor, old_rows), product(old_rows, old_rows)), "col"
    )
    reduced = eri_cols - old_cross
    reduced_rows = eri_rows - old_gram
    pivot_parts = []
    for step in range(steps):
        lo_col = step * width
        columns = reduced[:, lo_col : lo_col + width]
        column_rows = reduced_rows[:, lo_col : lo_col + width]
        if step > 0:
            earlier = jnp.concatenate(outputs, axis=1)
            earlier_rows = jnp.concatenate(pivot_parts, axis=1)
            own_rows = earlier_rows[lo_col : lo_col + width]
            columns = columns - product(earlier, own_rows)
            column_rows = column_rows - product(earlier_rows, own_rows)
        factor_block = jnp.linalg.cholesky(column_rows[lo_col : lo_col + width])
        new_panel = solve_panel(factor_block, columns)
        pivot_parts.append(solve_panel(factor_block, column_rows))
        diagonal = diagonal - jnp.sum(new_panel * new_panel, axis=1)
        outputs.append(new_panel)
    return (jnp.concatenate(outputs, axis=1), diagonal)


def solution(mesh):
    placed = (P("row", None), P("row", "col"), P("row"), P(), P("row"))
    return jax.shard_map(
        on_device, mesh=mesh, in_specs=placed, out_specs=(P("row", None), P("row")), check_vma=False
    )
```

profile of v0, /device:TPU:0, one launch (start us, length us, event | category | flops | bytes accessed | tf_op | source)
XLA Modules:
  0.0 291.3 jit_solution(2490053212816142319)
XLA Ops:
  7.2 1.0 compare_reduce_fusion
  8.3 0.2 fusion
  8.6 2.3 gather_fusion.1
  10.9 1.6 copy.20
  12.6 2.3 gather_fusion
  14.9 2.5 copy.19
  17.5 2.8 select_select_fusion.1
  20.3 0.2 all-reduce.7.cloned.1.call-start
  20.5 129.3 %all-reduce.5.cloned.1.call-done = (f32[512,512]{0,1:T(8,128)}, f32[512,512]{0,1:T(8,128)}) async-done(((f32[512,512]{0,1:T(8,128)}, f32[512,512]{0,1:T(8,128)}), (f32[512,512]{0,1:T(8,128)}, f32[512,512]{0,1:T(8,128)})) %all-reduce.5.cloned.1.call-update) | async-done | bytes 2097168 | tf_op jit(solution)/shard_map/psum | solution.py:35
  149.8 5.8 %convolution_bitcast_fusion = f32[512,512]{0,1:T(8,128)} fusion(f32[512,512]{0,1:T(8,128)} %get-tuple-element.9, f32[512,512]{1,0:T(8,128)S(1)} %copy-done), kind=kOutput, calls=%fused_computation.2 | convolution fusion | flops 1610612736 | bytes 3145728 | tf_op jit(solution)/shard_map/dot_general | solution.py:17
  155.6 2.9 fusion.41
  158.5 1.3 copy.23
  159.8 19.4 %all-reduce.7.cloned.1.call-done = (f32[512,512]{0,1:T(8,128)}, f32[512,512]{0,1:T(8,128)}) async-done(((f32[512,512]{0,1:T(8,128)}, f32[512,512]{0,1:T(8,128)}), (f32[512,512]{0,1:T(8,128)}, f32[512,512]{0,1:T(8,128)})) %all-reduce.7.cloned.1.call-update) | async-done | bytes 2097168 | tf_op jit(solution)/shard_map/psum | solution.py:36
  179.2 1.7 sub.36
  181.1 11.7 %cholesky.74 = f32[128,128]{1,0:T(8,128)S(1)} custom-call(f32[128,128]{1,0:T(8,128)S(1)} %fusion.34), custom_call_target="Cholesky" | custom-call | tf_op jit(solution)/shard_map/jit(cholesky)/cholesky | solution.py:52
  192.9 0.6 compare_reduce_fusion.4
  193.5 0.7 fusion.20
  194.2 9.8 %custom-call.11 = f32[1,128,128]{1,2,0:T(8,128)S(1)} custom-call(f32[1,128,128]{2,1,0:T(8,128)S(1)} %fusion.20), custom_call_target="InvertDiagBlocksLowerTriangular" | custom-call | tf_op jit(solution)/shard_map/triangular_solve/custom-call.0 | solution.py:23
  204.0 0.6 convolution_bitcast_fusion.6
  204.6 0.4 convolution_subtract_fusion.3
  205.2 11.7 %cholesky.85 = f32[128,128]{1,0:T(8,128)S(1)} custom-call(f32[128,128]{1,0:T(8,128)S(1)} %fusion.31), custom_call_target="Cholesky" | custom-call | tf_op jit(solution)/shard_map/jit(cholesky)/cholesky | solution.py:52
  216.9 0.6 compare_reduce_fusion.3
  217.6 0.7 fusion.21
  218.3 9.8 %custom-call.13 = f32[1,128,128]{1,2,0:T(8,128)S(1)} custom-call(f32[1,128,128]{2,1,0:T(8,128)S(1)} %fusion.21), custom_call_target="InvertDiagBlocksLowerTriangular" | custom-call | tf_op jit(solution)/shard_map/triangular_solve/custom-call.0 | solution.py:23
  228.1 0.4 convolution_bitcast_fusion.4
  228.5 0.5 convolution_subtract_fusion.1
  229.1 11.7 %cholesky.96 = f32[128,128]{1,0:T(8,128)S(1)} custom-call(f32[128,128]{1,0:T(8,128)S(1)} %fusion.28), custom_call_target="Cholesky" | custom-call | tf_op jit(solution)/shard_map/jit(cholesky)/cholesky | solution.py:52
  240.9 0.6 compare_reduce_fusion.2
  241.5 0.7 fusion.22
  242.2 10.0 %custom-call.15 = f32[1,128,128]{1,2,0:T(8,128)S(1)} custom-call(f32[1,128,128]{2,1,0:T(8,128)S(1)} %fusion.22), custom_call_target="InvertDiagBlocksLowerTriangular" | custom-call | tf_op jit(solution)/shard_map/triangular_solve/custom-call.0 | solution.py:23
  252.2 0.4 convolution_bitcast_fusion.2
  252.7 0.7 fusion.1
  253.4 0.2 slice-done
  253.7 11.7 %cholesky.107 = f32[128,128]{1,0:T(8,128)S(1)} custom-call(f32[128,128]{1,0:T(8,128)S(1)} %fusion.25), custom_call_target="Cholesky" | custom-call | tf_op jit(solution)/shard_map/jit(cholesky)/cholesky | solution.py:52
  265.5 0.6 compare_reduce_fusion.1
  266.1 0.7 fusion.23
  266.8 9.8 %custom-call.17 = f32[1,128,128]{1,2,0:T(8,128)S(1)} custom-call(f32[1,128,128]{2,1,0:T(8,128)S(1)} %fusion.23), custom_call_target="InvertDiagBlocksLowerTriangular" | custom-call | tf_op jit(solution)/shard_map/triangular_solve/custom-call.0 | solution.py:23
  276.6 1.4 sub.37
  278.0 0.4 multiply_reduce_fusion.3
  278.5 0.4 convolution_subtract_fusion.2
  278.9 0.4 multiply_reduce_fusion.2
  279.3 0.5 convolution_subtract_fusion
  279.8 0.4 multiply_reduce_fusion.1
  280.3 0.7 convolution_subtract_fusion.4
  281.0 0.4 multiply_reduce_fusion
  281.5 1.3 copy.30
  282.8 0.7 copy-done.7
  283.5 0.6 subtract_subtract_fusion
  (39 shorter events, 0.8 us)
Async XLA Ops:
  7.2 1.4 copy-start
  7.2 142.6 %all-reduce.5.cloned.1.call-start = ((), (), s32[]{:S(2)}) async-start(), calls=%async_computation | async-start | bytes 4194304 | tf_op jit(solution)/shard_map/psum | solution.py:35
  7.2 1.0 copy-start.5
  7.2 1.0 copy-start.6
  10.9 1.7 copy-start.1
  20.3 158.9 %all-reduce.7.cloned.1.call-start = ((), (), s32[]{:S(2)}) async-start(), calls=%async_computation.1 | async-start | bytes 4194304 | tf_op jit(solution)/shard_map/psum | solution.py:36
  149.8 5.8 %copy-start.2 = (f32[512,512]{0,1:T(8,128)S(1)}, f32[512,512]{0,1:T(8,128)}, u32[]{:S(2)}) copy-start(f32[512,512]{0,1:T(8,128)} %get-tuple-element.9) | copy-start | bytes 3145732
  181.0 47.5 %copy-start.3 = (f32[512,512]{0,1:T(8,128)}, f32[512,512]{0,1:T(8,128)S(1)}, u32[]{:S(2)}) copy-start(f32[512,512]{0,1:T(8,128)S(1)} %sub.36) | copy-start | bytes 3145732
  252.6 1.0 slice-start
  252.7 23.9 %copy-start.4 = (f32[512,512]{0,1:T(8,128)S(1)}, f32[512,512]{0,1:T(8,128)}, u32[]{:S(2)}) copy-start(f32[512,512]{0,1:T(8,128)} %copy.23) | copy-start | bytes 3145732
  282.8 0.7 copy-start.7
Sparse Core Ops, SparseCore 0:
  20.4 129.3 all-reduce.4
  158.6 20.5 all-reduce.6
where the time goes:
time: 294 us; the launch traced here: 291 us
  waiting for transfers between devices  149 us (51%)
  other arithmetic  99.7 us (34%)
  matrix products  15 us (5%)
  between operations  14.9 us (5%)
  local copies, waits for them, and re-layouts  12.8 us (4%)
    psum x1, waiting for transfers between devices, on_device(): old_rows, eri_rows = lax.psum((old_rows, eri_rows), 'row')  129 us
    another operation x12, other arithmetic, on_device(): factor_block = jnp.linalg.cholesky(column_rows[lo_col:lo_col + width])  49.6 us
    another operation x8, other arithmetic, solve_panel(): lax.linalg.triangular_solve(factor_block, columns, left_side=False, lower...  42.1 us
    psum x1, waiting for transfers between devices, on_device(): lax.psum((product(old_factor, old_rows), product(old_rows, old_rows)), 'c...  19.4 us
    dot_general x8, matrix products, product(): jnp.dot(left, right.T, precision=lax.Precision.HIGHEST, preferred_element...  11.8 us
    gather x4, local copies, waits for them, and re-layouts, pick_rows(): jnp.take(source, slots, axis=0)  8.84 us
  transfers between devices with their start and end apart: 2, of which 2 were waited for; matrix products, arithmetic and copies ran while one was open for 0% of the time, Pallas kernels for 0%

commit v1 on v0

v1 whole, which is shorter than its diff:
```python
import functools
import jax
import jax.numpy as jnp
from jax import lax
from jax.experimental import pallas as pl
from jax.experimental.pallas import tpu as pltpu
from jax.sharding import PartitionSpec as P

ROWS_T = (((1,), (1,)), ((), ()))
SUB = 8


def split(x):
    hi = x.astype(jnp.bfloat16)
    return hi, (x - hi.astype(jnp.float32)).astype(jnp.bfloat16)


def dot_t(a, b):
    f = functools.partial(
        lax.dot_general, dimension_numbers=ROWS_T, preferred_element_type=jnp.float32
    )
    return f(a[0], b[0]) + (f(a[0], b[1]) + f(a[1], b[0]))


def inverse_factor(a):
    n = a.shape[0]
    groups = n // SUB
    row = lax.broadcasted_iota(jnp.int32, (SUB, n), 0)
    lane = lax.broadcasted_iota(jnp.int32, (SUB, n), 1)
    A = [a[SUB * i : SUB * i + SUB, :] for i in range(groups)]
    W = [jnp.where(lane == row + SUB * i, 1.0, 0.0) for i in range(groups)]
    out = []
    wide = lambda v: jnp.broadcast_to(v, (SUB, n))
    for g in range(groups):
        j = SUB * g
        C = [[wide(A[i][:, j + k : j + k + 1]) for k in range(SUB)] for i in range(g, groups)]
        D = [[wide(C[0][l][k : k + 1, :]) for l in range(k + 1)] for k in range(SUB)]
        r = [wide(A[g][k : k + 1, :]) for k in range(SUB)]
        w = [wide(W[g][k : k + 1, :]) for k in range(SUB)]
        inv, m = [], [[None] * SUB for _ in range(SUB)]
        done = jnp.zeros((SUB, n), jnp.float32)
        for k in range(SUB):
            root = lax.rsqrt(D[k][k])
            inv.append(root * root)
            done = jnp.where(row == k, w[k] * root, done)
            for i in range(k + 1, SUB):
                m[i][k] = D[i][k] * inv[k]
            for i in range(k + 1, SUB):
                for l in range(k + 1, i + 1):
                    D[i][l] = D[i][l] - m[i][k] * D[l][k]
                r[i] = r[i] - m[i][k] * r[k]
                w[i] = w[i] - m[i][k] * w[k]
        out.append(done)
        if g + 1 == groups:
            break
        s, t = [None] * SUB, [None] * SUB
        for k in reversed(range(SUB)):
            s[k], t[k] = r[k] * inv[k], w[k] * inv[k]
            for i in reversed(range(k + 1, SUB)):
                s[k] = s[k] - m[i][k] * s[i]
                t[k] = t[k] - m[i][k] * t[i]
        for i in range(g + 1, groups):
            c = C[i - g]
            for k in range(SUB):
                A[i] = A[i] - c[k] * s[k]
                W[i] = W[i] - c[k] * t[k]
    return jnp.concatenate(out, axis=0)


def factor_kernel(steps, pivot_ref, rows_ref, diag_ref, panel_ref, new_ref, work):
    piv = pivot_ref.shape[0]
    width = piv // steps
    work[:piv, :] = pivot_ref[...]
    work[piv:, :] = rows_ref[...]
    new_ref[...] = diag_ref[...]
    ones = jnp.ones((SUB, width), jnp.bfloat16)

    def step(s, carry):
        at = pl.ds(pl.multiple_of(s * width, width), width)
        inv = split(inverse_factor(work[at, at]))
        solved = dot_t(split(work[:, at]), inv)
        own = solved[piv:]
        panel_ref[:, at] = own
        hi, lo = split(own * own)
        f = functools.partial(
            lax.dot_general, dimension_numbers=ROWS_T, preferred_element_type=jnp.float32
        )
        new_ref[...] -= (f(ones, hi) + f(ones, lo))[:1]

        @pl.when(s < steps - 1)
        def _():
            both = split(solved)
            work[...] -= dot_t(both, (both[0][:piv], both[1][:piv]))

        return carry

    lax.fori_loop(0, steps, step, 0)


def factor(pivot_rows, reduced, diagonal, steps):
    piv, rows = pivot_rows.shape[0], reduced.shape[0]
    panels, new = pl.pallas_call(
        functools.partial(factor_kernel, steps),
        out_shape=(
            jax.ShapeDtypeStruct((rows, piv), jnp.float32),
            jax.ShapeDtypeStruct((1, rows), jnp.float32),
        ),
        in_specs=[pl.BlockSpec(memory_space=pltpu.VMEM)] * 3,
        out_specs=[pl.BlockSpec(memory_space=pltpu.VMEM)] * 2,
        scratch_shapes=[pltpu.VMEM((piv + rows, piv), jnp.float32)],
        compiler_params=pltpu.CompilerParams(vmem_limit_bytes=40 * 1024 * 1024),
        name="factor",
    )(pivot_rows, reduced, diagonal[None, :])
    return panels, new[0]


def pick_rows(wanted, row_ids, arrays):
    matches = wanted[:, None] == row_ids[None, :]
    slots = jnp.sum(
        jnp.where(matches, lax.broadcasted_iota(jnp.int32, matches.shape, 1), 0), axis=1
    )
    present = jnp.any(matches, axis=1)[:, None]
    return tuple((jnp.where(present, jnp.take(source, slots, axis=0), 0.0) for source in arrays))


def product(left, right):
    return jnp.dot(
        left, right.T, precision=lax.Precision.HIGHEST, preferred_element_type=jnp.float32
    )


def on_device(eri_cols, old_factor, residual_diag, pivots, row_ids):
    every_pivot = pivots.reshape(-1)
    old_rows, eri_rows = pick_rows(every_pivot, row_ids, (old_factor, eri_cols))
    old_rows, eri_rows = lax.psum((old_rows, eri_rows), "row")
    old_cross, old_gram = lax.psum(
        (product(old_factor, old_rows), product(old_rows, old_rows)), "col"
    )
    return factor(
        eri_rows - old_gram, eri_cols - old_cross, residual_diag, pivots.shape[0]
    )


def solution(mesh):
    placed = (P("row", None), P("row", "col"), P("row"), P(), P("row"))
    return jax.shard_map(
        on_device, mesh=mesh, in_specs=placed, out_specs=(P("row", None), P("row")), check_vma=False
    )
```

time: 294 us -> 209 us (0.71)
  other arithmetic: 99.7 us -> 5.92 us
  Pallas kernels: 0 us -> 26.8 us
  local copies, waits for them, and re-layouts: 12.8 us -> 4.71 us
  matrix products: 15 us -> 6.99 us
    another operation x20 -> x0, other arithmetic: 91.6 us -> none  [the longest x12 49.6 us: on_device(): factor_block = jnp.linalg.cholesky(column_rows[lo_col:lo_col + width])]
    pallas_call x0 -> x1, Pallas kernels: none -> 26.8 us  [factor(): pl.pallas_call(functools.partial(factor_kernel, steps), out_shape=(jax.Sh...]
    gather x4 -> x2, local copies, waits for them, and re-layouts: 8.84 us -> 3.95 us  [pick_rows(): jnp.take(source, slots, axis=0)]
    dot_general x8 -> x2, matrix products: 11.8 us -> 6.99 us  [product(): jnp.dot(left, right.T, precision=lax.Precision.HIGHEST, preferred_element...]
    another operation x7 -> x0, matrix products: 3.23 us -> none  [solve_panel(): lax.linalg.triangular_solve(factor_block, columns, left_side=False, lower...]
where the time goes in v1:
time: 209 us
  waiting for transfers between devices  150 us (72%)
  Pallas kernels  26.8 us (13%)
  between operations  14.1 us (7%)
  matrix products  6.99 us (3%)
  other arithmetic  5.92 us (3%)
  local copies, waits for them, and re-layouts  4.71 us (2%)
    psum x1, waiting for transfers between devices, on_device(): old_rows, eri_rows = lax.psum((old_rows, eri_rows), 'row')  130 us
    pallas_call x1, Pallas kernels, factor(): pl.pallas_call(functools.partial(factor_kernel, steps), out_shape=(jax.Sh...  26.8 us
    psum x1, waiting for transfers between devices, on_device(): lax.psum((product(old_factor, old_rows), product(old_rows, old_rows)), 'c...  20.8 us
    dot_general x2, matrix products, product(): jnp.dot(left, right.T, precision=lax.Precision.HIGHEST, preferred_element...  6.99 us
  transfers between devices with their start and end apart: 2, of which 2 were waited for; matrix products, arithmetic and copies ran while one was open for 0% of the time, Pallas kernels for 0%

profile of v1, /device:TPU:0, one launch (start us, length us, event | category | flops | bytes accessed | tf_op | source)
XLA Modules:
  0.0 208.9 jit_solution(11960649120760344466)
XLA Ops:
  7.2 0.0 copy-start
  7.2 0.0 all-reduce.5.cloned.1.call-start
  7.2 0.0 copy-start.6
  7.2 0.0 copy-start.7
  7.2 1.0 compare_reduce_fusion
  8.3 0.0 copy-done.6
  8.3 0.0 copy-done.7
  8.3 0.2 fusion
  8.6 0.0 copy-done
  8.6 0.0 copy-start.2
  8.6 1.6 gather_fusion.1
  10.2 0.0 copy-done.2
  10.2 2.3 %gather_fusion = f32[512,512]{1,0:T(8,128)} fusion(f32[512,512]{1,0:T(8,128)S(1)} %copy-done.2, s32[1024]{0:T(1024)S(1)} %pad_clamp_fusion), kind=kCustom, calls=%fused_computation.clone | custom fusion | bytes 2099200 | tf_op jit(solution)/shard_map/jit(_take)/gather | solution.py:123
  12.6 2.8 %select_select_fusion = (f32[512,512]{1,0:T(8,128)}, f32[512,512]{1,0:T(8,128)}) fusion(f32[512,512]{1,0:T(8,128)S(1)} %gather_fusion.1, pred[512]{0:T(512)(128)(4,1)S(1)} %compare_and_fusion, pred[512]{0:T(512)(128)(4,1)S(1)} %compare_reduce_fusion, f32[512,512]{1,0:T(8,128)} %gather_fusion), kind=kLoop, calls=%fused_computation.6 | loop fusion | flops 1048576 | bytes 4195328 | tf_op jit(solution)/shard_map/jit(_where)/select_n | solution.py:123
  15.4 0.0 all-reduce.5.cloned.1.call-update
  15.4 0.0 all-reduce.7.cloned.1.call-start
  15.5 129.5 %all-reduce.5.cloned.1.call-done = (f32[512,512]{1,0:T(8,128)}, f32[512,512]{1,0:T(8,128)}) async-done(((f32[512,512]{1,0:T(8,128)}, f32[512,512]{1,0:T(8,128)}), (f32[512,512]{1,0:T(8,128)}, f32[512,512]{1,0:T(8,128)})) %all-reduce.5.cloned.1.call-update) | async-done | bytes 2097168 | tf_op jit(solution)/shard_map/psum | solution.py:135
  145.0 0.0 copy-start.3
  145.0 4.2 %convolution_bitcast_fusion = f32[512,512]{1,0:T(8,128)} fusion(f32[512,512]{1,0:T(8,128)} %get-tuple-element.8, f32[512,512]{1,0:T(8,128)S(1)} %copy-done), kind=kOutput, calls=%fused_computation.2 | convolution fusion | flops 1610612736 | bytes 3145728 | tf_op jit(solution)/shard_map/dot_general | solution.py:127
  149.1 0.0 copy-done.3
  149.1 2.8 %fusion.1 = f32[512,512]{1,0:T(8,128)} fusion(f32[512,512]{1,0:T(8,128)S(1)} %copy-done.3), kind=kOutput, calls=%fused_computation.11 | convolution fusion | flops 1610612736 | bytes 2097152 | tf_op jit(solution)/shard_map/dot_general | solution.py:127
  152.0 0.0 all-reduce.7.cloned.1.call-update
  152.0 20.8 %all-reduce.7.cloned.1.call-done = (f32[512,512]{1,0:T(8,128)}, f32[512,512]{1,0:T(8,128)}) async-done(((f32[512,512]{1,0:T(8,128)}, f32[512,512]{1,0:T(8,128)}), (f32[512,512]{1,0:T(8,128)}, f32[512,512]{1,0:T(8,128)})) %all-reduce.7.cloned.1.call-update) | async-done | bytes 2097168 | tf_op jit(solution)/shard_map/psum | solution.py:136
  172.8 0.0 copy-start.4
  172.8 0.0 copy-start.5
  172.8 1.6 sub.7.rows_ref
  174.4 0.0 copy-done.4
  174.4 0.3 copy-done.5
  174.6 0.0 copy-start.1
  174.6 0.2 sub.6.pivot_ref
  174.8 0.5 copy-done.1
  175.3 26.8 %factor.1 = (f32[512,512]{1,0:T(8,128)}, f32[1,512]{1,0:T(1,128)}) custom-call(f32[512,512]{1,0:T(8,128)S(1)} %sub.6.pivot_ref, f32[512,512]{1,0:T(8,128)S(1)} %sub.7.rows_ref, f32[1,512]{1,0:T(1,128)S(1)} %bitcast.9), custom_call_target="tpu_custom_call" | custom-call | tf_op jit(solution)/shard_map/factor/pallas_call | solution.py:102
  (3 shorter events, 0.0 us)
Async XLA Ops:
  7.2 1.4 copy-start
  7.2 137.8 %all-reduce.5.cloned.1.call-start = ((), (), s32[]{:S(2)}) async-start(), calls=%async_computation | async-start | bytes 4194304 | tf_op jit(solution)/shard_map/psum | solution.py:135
  7.2 1.0 copy-start.6
  7.2 1.0 copy-start.7
  8.6 1.6 copy-start.2
  15.4 157.3 %all-reduce.7.cloned.1.call-start = ((), (), s32[]{:S(2)}) async-start(), calls=%async_computation.1 | async-start | bytes 4194304 | tf_op jit(solution)/shard_map/psum | solution.py:136
  145.0 4.2 %copy-start.3 = (f32[512,512]{1,0:T(8,128)S(1)}, f32[512,512]{1,0:T(8,128)}, u32[]{:S(2)}) copy-start(f32[512,512]{1,0:T(8,128)} %get-tuple-element.8) | copy-start | bytes 3145732
  172.8 1.6 copy-start.4
  172.8 1.9 copy-start.5
  174.6 0.7 copy-start.1
Sparse Core Ops, SparseCore 0:
  15.6 129.3 all-reduce.4
  152.1 20.5 all-reduce.6
